TPU v7x, 32 devices: a whole 2x2x4 slice. The times are simulated.
32 devices in a mesh: grp: 2 (over y), row: 4 (over x, core), col: 4 (over z).
Axes of the slice: x: 2, y: 2, z: 4, core: 2. Of those that a mesh axis runs over, the one named last changes fastest.
Arguments:
- perturbation: bfloat16 [4, 12000, 12000], P('grp', 'row', 'col'), parts along dimension 0, may hold values from -96 to 96
- occ_coeffs: bfloat16 [12000, 2000], P('row', 'col'), may hold values from -0.0546875 to 0.0546875
- vir_coeffs: bfloat16 [12000, 512], P('col', 'row'), may hold values from -0.0546875 to 0.0546875
- occ_energies: float32 [2000], replicated, may hold values from -1 to -0.1
- vir_energies: float32 [512], replicated, may hold values from 0.1 to 1.5
Outputs:
- density_response: bfloat16 [4, 12000, 12000], P('grp', 'row', 'col'), parts along dimension 0
There are 2 independent parts, one for each index of `grp`. A program takes and returns all parts, laid end to end along the dimension named above; an argument that names none is the same for every part. Nothing has to cross between parts.
All inputs are finite; a program needn't handle non-finite values.
Results may differ from a plain program's by a relative error of at most 0.0098.
Values may be sent and summed in bfloat16 or wider, within the bound.
A program may use at most 192 MiB of HBM per device.

v0:
```python
import jax
import jax.numpy as jnp
from jax import lax
from jax.sharding import PartitionSpec as P

BF16 = jnp.bfloat16
F32 = jnp.float32


def per_device(perturbation, occ_coeffs, vir_coeffs, occ_energies, vir_energies):
    vir_rows = lax.all_gather(vir_coeffs, "row", axis=1, tiled=True)
    occ_parts = lax.all_gather(occ_coeffs, "col")
    cols, _, width = occ_parts.shape
    image = jnp.einsum("pij,jv->piv", perturbation, vir_rows, preferred_element_type=F32).astype(
        BF16
    )
    part = jnp.einsum("cio,piv->pcov", occ_parts, image, preferred_element_type=F32).astype(BF16)
    coupling = lax.psum(part, ("row", "col"))
    gaps = occ_energies.reshape(cols, width)[:, :, None] - vir_energies[None, None, :]
    response = (coupling.astype(F32) / gaps[None]).astype(BF16)
    mixed = jnp.einsum("cio,pcov->piv", occ_parts, response, preferred_element_type=F32).astype(
        BF16
    )
    return jnp.einsum("piv,jv->pij", mixed, vir_rows, preferred_element_type=F32).astype(BF16)


def solution(mesh):
    placed = (P("grp", "row", "col"), P("row", "col"), P("col", "row"), P(), P())
    return jax.shard_map(
        per_device, mesh=mesh, in_specs=placed, out_specs=P("grp", "row", "col"), check_vma=False
    )
```

profile of v0, /device:TPU:0, one launch (start us, length us, event | category | flops | bytes accessed | tf_op | source)
XLA Modules:
  0.0 448.0 jit_solution(10581064769501468559)
XLA Ops:
  6.5 0.0 all-gather.4.cloned.1.call-start
  6.5 0.7 all-gather.4.cloned.1.call-update
  7.3 0.0 all-gather.6.cloned.1.call-start
  7.3 0.7 all-gather.6.cloned.1.call-update
  8.0 0.0 all-reduce.2.cloned.1.call-start
  8.1 32.1 %all-gather.4.cloned.1.call-done = bf16[3000,512]{1,0:T(8,128)(2,1)} async-done(((bf16[3000,128]{1,0:T(8,128)(2,1)}), bf16[3000,512]{1,0:T(8,128)(2,1)}) %all-gather.4.cloned.1.call-update) | async-done | bytes 3072016 | tf_op jit(solution)/shard_map/all_gather | solution.py:11
  40.1 25.8 %fusion.45 = bf16[2,3000,512,1]{2,1,3,0:T(8,128)(2,1)} fusion(bf16[2,3000,3000]{2,1,0:T(8,128)(2,1)} %param.5, bf16[3000,512]{1,0:T(8,128)(2,1)} %all-gather.4.cloned.1.call-done), kind=kOutput, calls=%fused_computation.5.clone.clone.clone.1 | convolution fusion | flops 18435072000 | bytes 45216000 | tf_op jit(solution)/shard_map/pij,jv->piv/dot_general | solution.py:14
  66.0 189.1 %all-gather.6.cloned.1.call-done = bf16[12000,500]{1,0:T(8,128)(2,1)} async-done(((bf16[3000,500]{1,0:T(8,128)(2,1)}), bf16[12000,500]{1,0:T(8,128)(2,1)}) %all-gather.6.cloned.1.call-update) | async-done | bytes 12000016 | tf_op jit(solution)/shard_map/all_gather | solution.py:12
  255.1 19.1 %fusion.17 = bf16[2,512,4,500]{1,3,2,0:T(8,128)(2,1)} fusion(bf16[4,3000,500,1]{2,1,0,3:T(8,128)(2,1)} %bitcast.58, bf16[2,3000,512,1]{2,1,3,0:T(8,128)(2,1)} %fusion.45), kind=kOutput, calls=%fused_computation.12 | convolution fusion | flops 12290048000 | bytes 22240000 | tf_op jit(solution)/shard_map/cio,piv->pcov/dot_general | solution.py:17
  274.2 0.0 copy-start
  274.2 0.0 copy-start.1
  274.2 7.8 %copy.10 = bf16[2,512,4,500]{3,2,1,0:T(4,128)(2,1)} copy(bf16[2,512,4,500]{1,3,2,0:T(8,128)(2,1)} %fusion.17) | data formatting | bytes 8192000
  282.0 0.0 all-reduce.2.cloned.1.call-update
  282.0 0.0 copy-done
  282.1 0.1 sub.19
  282.1 0.0 copy-done.1
  282.1 2.8 broadcast_subtract_fusion
  285.0 106.6 %all-reduce.2.cloned.1.call-done = bf16[2,4,500,512]{2,1,3,0:T(4,128)(2,1)} async-done(((bf16[2,4,500,512]{2,1,3,0:T(4,128)(2,1)}), bf16[2,4,500,512]{2,1,3,0:T(4,128)(2,1)}) %all-reduce.2.cloned.1.call-update) | async-done | bytes 4096016 | tf_op jit(solution)/shard_map/psum | solution.py:18
  391.5 5.5 %fusion = bf16[2,4,500,512]{2,1,3,0:T(4,128)(2,1)S(1)} fusion(bf16[2,4,500,512]{2,1,3,0:T(4,128)(2,1)} %all-reduce.2.cloned.1.call-done, f32[4,500,512]{1,0,2:T(4,128)} %broadcast_subtract_fusion), kind=kLoop, calls=%fused_computation.3 | loop fusion | flops 6144000 | bytes 12288000 | tf_op jit(solution)/shard_map/convert_element_type | solution.py:20
  397.1 16.8 %fusion.41 = bf16[2,3000,512]{2,1,0:T(8,128)(2,1)} fusion(bf16[4,3000,500,1]{2,1,0,3:T(8,128)(2,1)} %bitcast.59, bf16[2,4,500,512]{2,1,3,0:T(4,128)(2,1)S(1)} %fusion), kind=kOutput, calls=%fused_computation.6.clone.1 | convolution fusion | flops 12291072000 | bytes 22240000 | tf_op jit(solution)/shard_map/cio,pcov->piv/dot_general | solution.py:21
  413.9 27.6 %convolution_convert_fusion = bf16[2,3000,3000]{2,1,0:T(8,128)(2,1)} fusion(bf16[3000,512]{1,0:T(8,128)(2,1)} %all-gather.4.cloned.1.call-done, bf16[2,3000,512]{2,1,0:T(8,128)(2,1)} %fusion.41), kind=kOutput, calls=%fused_computation | convolution fusion | flops 18449999872 | bytes 45216000 | tf_op jit(solution)/shard_map/piv,jv->pij/dot_general | solution.py:24
Async XLA Ops:
  6.5 33.6 %all-gather.4.cloned.1.call-start = ((), (), s32[]{:S(2)}) async-start(), calls=%async_computation | async-start | bytes 3840000 | tf_op jit(solution)/shard_map/all_gather | solution.py:11
  7.3 247.8 %all-gather.6.cloned.1.call-start = ((), (), s32[]{:S(2)}) async-start(), calls=%async_computation.2 | async-start | bytes 15360000 | tf_op jit(solution)/shard_map/all_gather | solution.py:12
  8.0 383.5 %all-reduce.2.cloned.1.call-start = ((), (), s32[]{:S(2)}) async-start(), calls=%async_computation.1 | async-start | bytes 8388608 | tf_op jit(solution)/shard_map/psum | solution.py:18
  274.2 7.9 %copy-start = (f32[2000]{0:T(1024)S(1)}, f32[2000]{0:T(1024)}, u32[]{:S(2)}) copy-start(f32[2000]{0:T(1024)} %param.8) | copy-start | bytes 24004
  274.2 8.0 %copy-start.1 = (f32[512]{0:T(512)S(1)}, f32[512]{0:T(512)}, u32[]{:S(2)}) copy-start(f32[512]{0:T(512)} %param.9) | copy-start | bytes 6148
Sparse Core Ops, SparseCore 0:
  8.9 31.1 all-gather.3
  41.7 213.3 all-gather.5
  282.2 109.3 all-reduce.1
where the time goes:
time: 448 us
  waiting for transfers between devices  329 us (73%)
  matrix products  89.4 us (20%)
  between operations  13.1 us (3%)
  other arithmetic  8.38 us (2%)
  local copies, waits for them, and re-layouts  7.93 us (2%)
    all_gather x1, waiting for transfers between devices, per_device(): occ_parts = lax.all_gather(occ_coeffs, 'col')  189 us
    psum x1, waiting for transfers between devices, per_device(): coupling = lax.psum(part, ('row', 'col'))  107 us
    all_gather x1, waiting for transfers between devices, per_device(): vir_rows = lax.all_gather(vir_coeffs, 'row', axis=1, tiled=True)  32.1 us
    dot_general x1, matrix products, per_device(): jnp.einsum('piv,jv->pij', mixed, vir_rows, preferred_element_type=F32)  27.6 us
    dot_general x1, matrix products, per_device(): jnp.einsum('pij,jv->piv', perturbation, vir_rows, preferred_element_type=...  25.8 us
    dot_general x1, matrix products, per_device(): jnp.einsum('cio,piv->pcov', occ_parts, image, preferred_element_type=F32)  19.1 us
    dot_general x1, matrix products, per_device(): jnp.einsum('cio,pcov->piv', occ_parts, response, preferred_element_type=F32)  16.8 us
  transfers between devices with their start and end apart: 3, of which 3 were waited for; matrix products, arithmetic and copies ran while one was open for 6% of the time, Pallas kernels for 0%

commit v1 on v0

--- a/solution.py
+++ b/solution.py
@@ -2,6 +2,7 @@
 import jax.numpy as jnp
 from jax import lax
 from jax.sharding import PartitionSpec as P
+from jax.lax import psum
 
 BF16 = jnp.bfloat16
 F32 = jnp.float32
@@ -15,7 +16,7 @@
         BF16
     )
     part = jnp.einsum("cio,piv->pcov", occ_parts, image, preferred_element_type=F32).astype(BF16)
-    coupling = lax.psum(part, ("row", "col"))
+    coupling = psum(psum(part, "row"), "col")
     gaps = occ_energies.reshape(cols, width)[:, :, None] - vir_energies[None, None, :]
     response = (coupling.astype(F32) / gaps[None]).astype(BF16)
     mixed = jnp.einsum("cio,pcov->piv", occ_parts, response, preferred_element_type=F32).astype(

time: 448 us -> 580 us (1.29)
  waiting for transfers between devices: 329 us -> 461 us
    psum x1 -> x2, waiting for transfers between devices: 107 us -> 238 us  [per_device(): coupling = psum(psum(part, 'row'), 'col')]
  transfers between devices with their start and end apart: 3 -> 4, of which waited for: 3 -> 4; matrix products, arithmetic and copies ran while one was open for 6% -> 5% of each run, Pallas kernels for 0% -> 0%
where the time goes in v1:
time: 580 us
  waiting for transfers between devices  461 us (79%)
  matrix products  89.4 us (15%)
  between operations  13.1 us (2%)
  other arithmetic  8.39 us (1%)
  local copies, waits for them, and re-layouts  7.9 us (1%)
    psum x2, waiting for transfers between devices, per_device(): coupling = psum(psum(part, 'row'), 'col')  238 us
    all_gather x1, waiting for transfers between devices, per_device(): occ_parts = lax.all_gather(occ_coeffs, 'col')  189 us
    all_gather x1, waiting for transfers between devices, per_device(): vir_rows = lax.all_gather(vir_coeffs, 'row', axis=1, tiled=True)  32.1 us
    dot_general x1, matrix products, per_device(): jnp.einsum('piv,jv->pij', mixed, vir_rows, preferred_element_type=F32)  27.6 us
    dot_general x1, matrix products, per_device(): jnp.einsum('pij,jv->piv', perturbation, vir_rows, preferred_element_type=...  25.8 us
    dot_general x1, matrix products, per_device(): jnp.einsum('cio,piv->pcov', occ_parts, image, preferred_element_type=F32)  19.1 us
    dot_general x1, matrix products, per_device(): jnp.einsum('cio,pcov->piv', occ_parts, response, preferred_element_type=F32)  16.8 us
  transfers between devices with their start and end apart: 4, of which 4 were waited for; matrix products, arithmetic and copies ran while one was open for 5% of the time, Pallas kernels for 0%

profile of v1, /device:TPU:0, one launch (start us, length us, event | category | flops | bytes accessed | tf_op | source)
XLA Modules:
  0.0 579.7 jit_solution(10620880097560044781)
XLA Ops:
  6.5 0.0 all-gather.4.cloned.1.call-start
  6.5 0.7 all-gather.4.cloned.1.call-update
  7.3 0.0 all-gather.6.cloned.1.call-start
  7.3 0.7 all-gather.6.cloned.1.call-update
  8.0 0.0 all-reduce.3.cloned.1.call-start
  8.1 32.1 %all-gather.4.cloned.1.call-done = bf16[3000,512]{1,0:T(8,128)(2,1)} async-done(((bf16[3000,128]{1,0:T(8,128)(2,1)}), bf16[3000,512]{1,0:T(8,128)(2,1)}) %all-gather.4.cloned.1.call-update) | async-done | bytes 3072016 | tf_op jit(solution)/shard_map/all_gather | solution.py:12
  40.1 25.8 %fusion.45 = bf16[2,3000,512,1]{2,1,3,0:T(8,128)(2,1)} fusion(bf16[2,3000,3000]{2,1,0:T(8,128)(2,1)} %param.5, bf16[3000,512]{1,0:T(8,128)(2,1)} %all-gather.4.cloned.1.call-done), kind=kOutput, calls=%fused_computation.5.clone.clone.clone.1 | convolution fusion | flops 18435072000 | bytes 45216000 | tf_op jit(solution)/shard_map/pij,jv->piv/dot_general | solution.py:15
  66.0 189.1 %all-gather.6.cloned.1.call-done = bf16[12000,500]{1,0:T(8,128)(2,1)} async-done(((bf16[3000,500]{1,0:T(8,128)(2,1)}), bf16[12000,500]{1,0:T(8,128)(2,1)}) %all-gather.6.cloned.1.call-update) | async-done | bytes 12000016 | tf_op jit(solution)/shard_map/all_gather | solution.py:13
  255.1 19.1 %fusion.17 = bf16[2,512,4,500]{1,3,2,0:T(8,128)(2,1)} fusion(bf16[4,3000,500,1]{2,1,0,3:T(8,128)(2,1)} %bitcast.58, bf16[2,3000,512,1]{2,1,3,0:T(8,128)(2,1)} %fusion.45), kind=kOutput, calls=%fused_computation.12 | convolution fusion | flops 12290048000 | bytes 22240000 | tf_op jit(solution)/shard_map/cio,piv->pcov/dot_general | solution.py:18
  274.2 7.8 %copy.10 = bf16[2,512,4,500]{3,2,1,0:T(4,128)(2,1)} copy(bf16[2,512,4,500]{1,3,2,0:T(8,128)(2,1)} %fusion.17) | data formatting | bytes 8192000
  282.0 0.0 copy-start
  282.0 0.0 copy-start.1
  282.0 0.0 all-reduce.3.cloned.1.call-update
  282.0 0.2 all-reduce.5.cloned.1.call-start
  282.2 83.6 %all-reduce.3.cloned.1.call-done = bf16[2,4,500,512]{2,1,3,0:T(4,128)(2,1)} async-done(((bf16[2,4,500,512]{2,1,3,0:T(4,128)(2,1)}), bf16[2,4,500,512]{2,1,3,0:T(4,128)(2,1)}) %all-reduce.3.cloned.1.call-update) | async-done | bytes 4096016 | tf_op jit(solution)/shard_map/psum | solution.py:19
  365.8 0.0 all-reduce.5.cloned.1.call-update
  365.8 0.0 copy-done
  365.9 0.1 sub.19
  365.9 0.0 copy-done.1
  365.9 2.8 broadcast_subtract_fusion
  368.8 154.4 %all-reduce.5.cloned.1.call-done = bf16[2,4,500,512]{2,1,3,0:T(4,128)(2,1)} async-done(((bf16[2,4,500,512]{2,1,3,0:T(4,128)(2,1)}), bf16[2,4,500,512]{2,1,3,0:T(4,128)(2,1)}) %all-reduce.5.cloned.1.call-update) | async-done | bytes 4096016 | tf_op jit(solution)/shard_map/psum | solution.py:19
  523.2 5.5 fusion
  528.8 16.8 %fusion.41 = bf16[2,3000,512]{2,1,0:T(8,128)(2,1)} fusion(bf16[4,3000,500,1]{2,1,0,3:T(8,128)(2,1)} %bitcast.59, bf16[2,4,500,512]{2,1,3,0:T(4,128)(2,1)S(1)} %fusion), kind=kOutput, calls=%fused_computation.6.clone.1 | convolution fusion | flops 12291072000 | bytes 22240000 | tf_op jit(solution)/shard_map/cio,pcov->piv/dot_general | solution.py:22
  545.6 27.6 %convolution_convert_fusion = bf16[2,3000,3000]{2,1,0:T(8,128)(2,1)} fusion(bf16[3000,512]{1,0:T(8,128)(2,1)} %all-gather.4.cloned.1.call-done, bf16[2,3000,512]{2,1,0:T(8,128)(2,1)} %fusion.41), kind=kOutput, calls=%fused_computation | convolution fusion | flops 18449999872 | bytes 45216000 | tf_op jit(solution)/shard_map/piv,jv->pij/dot_general | solution.py:25
Async XLA Ops:
  6.5 33.6 %all-gather.4.cloned.1.call-start = ((), (), s32[]{:S(2)}) async-start(), calls=%async_computation | async-start | bytes 3840000 | tf_op jit(solution)/shard_map/all_gather | solution.py:12
  7.3 247.8 %all-gather.6.cloned.1.call-start = ((), (), s32[]{:S(2)}) async-start(), calls=%async_computation.3 | async-start | bytes 15360000 | tf_op jit(solution)/shard_map/all_gather | solution.py:13
  8.0 357.8 %all-reduce.3.cloned.1.call-start = ((), (), s32[]{:S(2)}) async-start(), calls=%async_computation.1 | async-start | bytes 8388608 | tf_op jit(solution)/shard_map/psum | solution.py:19
  282.0 83.9 %copy-start = (f32[2000]{0:T(1024)S(1)}, f32[2000]{0:T(1024)}, u32[]{:S(2)}) copy-start(f32[2000]{0:T(1024)} %param.8) | copy-start | bytes 24004
  282.0 84.0 %copy-start.1 = (f32[512]{0:T(512)S(1)}, f32[512]{0:T(512)}, u32[]{:S(2)}) copy-start(f32[512]{0:T(512)} %param.9) | copy-start | bytes 6148
  282.0 241.2 %all-reduce.5.cloned.1.call-start = ((), (), s32[]{:S(2)}) async-start(), calls=%async_computation.2 | async-start | bytes 8388608 | tf_op jit(solution)/shard_map/psum | solution.py:19
Sparse Core Ops, SparseCore 0:
  8.9 31.1 all-gather.3
  41.7 213.3 all-gather.5
  282.1 83.6 all-reduce.2
  368.0 155.1 all-reduce.4
